TPU v7x, 32 devices: a whole 2x2x4 slice. The times are simulated.
32 devices in a mesh: dp: 8 (over z, x), seq: 4 (over y, core).
Axes of the slice: x: 2, y: 2, z: 4, core: 2. Of those that a mesh axis runs over, the one named last changes fastest.
Arguments:
- tokens: bfloat16 [4608, 3584], P('dp'), may hold values from -6 to 6
- positions: int32 [3, 4608], P(None, 'dp'), may hold values from 0 to 2047
- loss_mask: int32 [4608], P('dp'), may hold values from 0 to 1, as said below
- sample_tokens: int32 [8, 3], replicated, may hold values from 96 to 384, as said below
- dest_slot: int32 [4608], P('dp'), may hold values from 0 to 6143, as said below
- norm_gain: float32 [3584], replicated, may hold values from 0.5 to 1.5
- q_weight: bfloat16 [3584, 2048], P(None, 'seq'), may hold values from -0.09375 to 0.09375
- k_weight: bfloat16 [3584, 512], P(None, 'seq'), may hold values from -0.09375 to 0.09375
- v_weight: bfloat16 [3584, 512], P(None, 'seq'), may hold values from -0.09375 to 0.09375
- q_bias: float32 [2048], P('seq'), may hold values from -3 to 3
- k_bias: float32 [512], P('seq'), may hold values from -3 to 3
- v_bias: float32 [512], P('seq'), may hold values from -3 to 3
- o_weight: bfloat16 [2048, 3584], P('seq'), may hold values from -0.125 to 0.125
Outputs:
- mixed: bfloat16 [6144, 3584], P(('dp', 'seq'))
- token_weight: float32 [6144], P(('dp', 'seq'))
Inputs may be any that keep to these rules, and one draw needn't show every extreme that they name: `sample_tokens`: row r gives the token counts of the samples in the buckets of receiver r, of 384, 192 and 192 slots; each count lies between half of its bucket's slots and all of them. Some receiver has all three buckets full. All counts together equal the number of rows of tokens. `dest_slot`: every row has a slot of its own, and the slots that rows take are exactly the first sample_tokens[r, b] slots of each bucket b of each receiver r. Of the rows of one sender at most 96 go to one receiver; a receiver whose buckets are all full takes exactly 96 rows from every sender. `loss_mask`: the first of each sender's 576 rows is 1.
All inputs are finite; a program needn't handle non-finite values.
Results may differ from a plain program's by a relative error of at most 0.015.
Values may be sent and summed in bfloat16 or wider, within the bound.
A program may use at most 128 MiB of HBM per device.

v0:
```python
import math

import jax
import jax.numpy as jnp
from jax import lax
from jax.sharding import PartitionSpec as P

DH = 128
BUCKET = 384


NORM_EPSILON = 1e-06
ROPE_BASE = 1000000.0


def rms_norm(rows_in, gain):
    widened = rows_in.astype(jnp.float32)
    mean_square = jnp.mean(widened * widened, axis=-1, keepdims=True)
    return (widened * lax.rsqrt(mean_square + NORM_EPSILON) * gain).astype(jnp.bfloat16)


def rotary_tables(position_ids, head_size):
    half_size = head_size // 2
    pair_index = jnp.arange(half_size, dtype=jnp.int32)
    inv_freq = jnp.exp(pair_index.astype(jnp.float32) * (-2.0 * math.log(ROPE_BASE) / head_size))
    time_limit = head_size // 8
    height_limit = time_limit + 3 * head_size // 16
    chosen = jnp.where(
        pair_index[None, :] < time_limit,
        position_ids[0][:, None],
        jnp.where(
            pair_index[None, :] < height_limit, position_ids[1][:, None], position_ids[2][:, None]
        ),
    )
    angles = chosen.astype(jnp.float32) * inv_freq[None, :]
    return (jnp.cos(angles), jnp.sin(angles))


def rotate(heads_in, cosine, sine_part):
    half_size = heads_in.shape[-1] // 2
    first_half = heads_in[..., :half_size]
    second_half = heads_in[..., half_size:]
    cosine = cosine[:, None, :]
    sine_part = sine_part[:, None, :]
    return jnp.concatenate(
        [
            first_half * cosine - second_half * sine_part,
            second_half * cosine + first_half * sine_part,
        ],
        axis=-1,
    )


def project(normed, q_weight, k_weight, v_weight, q_bias, k_bias, v_bias):
    queries = (jnp.dot(normed, q_weight, preferred_element_type=jnp.float32) + q_bias).astype(
        jnp.bfloat16
    )
    key_rows = (jnp.dot(normed, k_weight, preferred_element_type=jnp.float32) + k_bias).astype(
        jnp.bfloat16
    )
    value_rows = (jnp.dot(normed, v_weight, preferred_element_type=jnp.float32) + v_bias).astype(
        jnp.bfloat16
    )
    return (queries, key_rows, value_rows)


def rotate_rows(queries, key_rows, position_ids):
    cosine, sine_part = rotary_tables(position_ids, DH)
    row_count = queries.shape[0]
    q_turned = rotate(queries.astype(jnp.float32).reshape(row_count, -1, DH), cosine, sine_part)
    k_turned = rotate(key_rows.astype(jnp.float32).reshape(row_count, -1, DH), cosine, sine_part)
    return (
        q_turned.astype(jnp.bfloat16).reshape(row_count, -1),
        k_turned.astype(jnp.bfloat16).reshape(row_count, -1),
    )


def place_rows(rows_in, target_slots, slot_count):
    flat_rows = rows_in.reshape(slot_count, -1)
    empty = jnp.zeros((slot_count, flat_rows.shape[-1]), flat_rows.dtype)
    return empty.at[target_slots].set(flat_rows, mode="drop")


def attend_group(queries, key_rows, value_rows, lengths):
    block_count = queries.shape[0]
    row_count = queries.shape[1]
    scores = jnp.einsum(
        "bqagd,bkad->bagqk", queries, key_rows, preferred_element_type=jnp.float32
    ) * (1.0 / math.sqrt(DH))
    places = jnp.arange(row_count, dtype=jnp.int32)
    allowed = (places[:, None] >= places[None, :])[None] & (
        places[None, None, :] < lengths[:, None, None]
    )
    scores = jnp.where(allowed[:, None, None], scores, -1e30)
    weights = jax.nn.softmax(scores, axis=-1).astype(jnp.bfloat16)
    context = jnp.einsum(
        "bagqk,bkad->bqagd", weights, value_rows, preferred_element_type=jnp.float32
    )
    live_rows = places[None, :] < lengths[:, None]
    context = jnp.where(live_rows[:, :, None, None, None], context, 0.0).astype(jnp.bfloat16)
    return context.reshape(block_count * row_count, -1)


def attend_buckets(q_rows, k_rows, v_rows, lengths, kv_count, group_size):
    half_bucket = BUCKET // 2
    first_part = attend_group(
        q_rows[:BUCKET].reshape(1, BUCKET, kv_count, group_size, DH),
        k_rows[:BUCKET].reshape(1, BUCKET, kv_count, DH),
        v_rows[:BUCKET].reshape(1, BUCKET, kv_count, DH),
        lengths[:1],
    )
    second_part = attend_group(
        q_rows[BUCKET:].reshape(2, half_bucket, kv_count, group_size, DH),
        k_rows[BUCKET:].reshape(2, half_bucket, kv_count, DH),
        v_rows[BUCKET:].reshape(2, half_bucket, kv_count, DH),
        lengths[1:],
    )
    return jnp.concatenate([first_part, second_part], axis=0)


def per_device(
    tokens,
    positions,
    loss_mask,
    sample_tokens,
    dest_slot,
    norm_gain,
    q_weight,
    k_weight,
    v_weight,
    q_bias,
    k_bias,
    v_bias,
    o_weight,
):
    peer_count = lax.axis_size("dp")
    own_index = lax.axis_index("dp")
    seq_count = lax.axis_size("seq")
    seq_index = lax.axis_index("seq")
    source_rows = tokens.shape[0]
    slot_count = 2 * BUCKET
    capacity = slot_count // peer_count
    head_count = q_weight.shape[1] // DH
    kv_count = k_weight.shape[1] // DH
    group_size = head_count // kv_count
    target_peer = dest_slot // slot_count
    target_local = dest_slot % slot_count
    peer_ids = jnp.arange(peer_count, dtype=jnp.int32)
    one_hot = (target_peer[:, None] == peer_ids[None, :]).astype(jnp.int32)
    ranking = jnp.sum((jnp.cumsum(one_hot, axis=0) - one_hot) * one_hot, axis=1)
    buffer_slot = target_peer * capacity + ranking
    row_ids = jnp.arange(source_rows, dtype=jnp.int32)
    source_of = jnp.zeros((slot_count,), jnp.int32).at[buffer_slot].set(row_ids)
    is_live = jnp.zeros((slot_count,), jnp.int32).at[buffer_slot].set(1) > 0
    info_rows = jnp.concatenate([positions, loss_mask[None, :], target_local[None, :]], axis=0)
    filler = jnp.array([0, 0, 0, 0, slot_count], jnp.int32)[:, None]
    send_info = jnp.where(is_live[None, :], info_rows[:, source_of], filler)
    mask_sum = jnp.sum(loss_mask)
    recv_info = lax.all_to_all(send_info, "dp", split_axis=1, concat_axis=1, tiled=True)
    loss_total = lax.psum(mask_sum.astype(jnp.float32), "dp")
    recv_local = recv_info[4]
    slot_info = (
        jnp.zeros((4, slot_count), jnp.int32).at[:, recv_local].set(recv_info[:4], mode="drop")
    )
    zero_value = jnp.zeros((), jnp.bfloat16)
    q_all, k_all, v_all = project(
        rms_norm(tokens, norm_gain), q_weight, k_weight, v_weight, q_bias, k_bias, v_bias
    )
    q_all, k_all = rotate_rows(q_all, k_all, positions)

    def select_slots(source_array):
        return jnp.where(is_live[:, None], source_array[source_of], zero_value).reshape(
            peer_count, capacity, -1
        )

    q_recv, k_recv, v_recv = (
        lax.all_to_all(select_slots(q_all), "dp", split_axis=0, concat_axis=0, tiled=True),
        lax.all_to_all(select_slots(k_all), "dp", split_axis=0, concat_axis=0, tiled=True),
        lax.all_to_all(select_slots(v_all), "dp", split_axis=0, concat_axis=0, tiled=True),
    )
    q_slots = place_rows(q_recv, recv_local, slot_count)
    k_slots = place_rows(k_recv, recv_local, slot_count)
    v_slots = place_rows(v_recv, recv_local, slot_count)
    lengths = sample_tokens[own_index]
    context = attend_buckets(q_slots, k_slots, v_slots, lengths, kv_count, group_size)
    part_rows = slot_count // seq_count
    mixed = lax.psum_scatter(
        jnp.dot(context, o_weight, preferred_element_type=jnp.float32).astype(jnp.bfloat16),
        "seq",
        scatter_dimension=0,
        tiled=True,
    )
    row_scale = peer_count * source_rows / loss_total
    own_mask = lax.dynamic_slice_in_dim(slot_info[3], seq_index * part_rows, part_rows, 0).astype(
        jnp.float32
    )
    return (mixed, own_mask * row_scale)


def solution(mesh):
    return jax.shard_map(
        per_device,
        mesh=mesh,
        in_specs=(
            P("dp", None),
            P(None, "dp"),
            P("dp"),
            P(),
            P("dp"),
            P(),
            P(None, "seq"),
            P(None, "seq"),
            P(None, "seq"),
            P("seq"),
            P("seq"),
            P("seq"),
            P("seq", None),
        ),
        out_specs=(P(("dp", "seq"), None), P(("dp", "seq"))),
        check_vma=False,
    )
```

profile of v0, /device:TPU:0, one launch (start us, length us, event | category | flops | bytes accessed | tf_op | source)
XLA Modules:
  0.0 176.1 jit_solution(11099056291222046183)
XLA Ops:
  7.2 0.8 broadcast_in_dim.220
  8.0 0.7 add_select_fusion.1
  8.7 1.4 reduce-window.6
  10.7 0.7 compare_select_fusion.2
  11.4 4.1 %scatter_custom_fusion = s32[768]{0:T(1024)S(1)} fusion(s32[576]{0:T(1024)S(1)} %get-tuple-element.13, s32[576]{0:T(1024)S(1)} %ne.22, s32[]{:T(128)} %constant.26.clone.1), kind=kCustom, calls=%fused_computation.110 | custom fusion | bytes 3076 | tf_op jit(solution)/shard_map/scatter | solution.py:154
  15.5 4.1 %scatter_custom_fusion.1 = s32[768]{0:T(1024)S(1)} fusion(s32[576]{0:T(1024)S(1)} %get-tuple-element.13, s32[576]{0:T(1024)S(1)} %iota.74, s32[]{:T(128)} %constant.26.clone.1), kind=kCustom, calls=%fused_computation.107 | custom fusion | bytes 3076 | tf_op jit(solution)/shard_map/scatter | solution.py:153
  19.7 0.7 pad_add_fusion
  20.6 1.6 gather_fusion
  22.4 0.7 fusion.55
  23.1 0.7 reshape.820
  23.8 7.3 %all-to-all-start = ((s32[8,1,480]{2,1,0:T(1,128)}), s32[8,1,480]{2,1,0:T(1,128)S(1)}, u32[]{:S(2)}, u32[]{:S(2)}) async-start(s32[8,1,480]{2,1,0:T(1,128)} %reshape.820), calls=%async_computation | async-start | bytes 32768 | tf_op jit(solution)/shard_map/all_to_all | solution.py:159
  31.1 0.9 slice_reduce_fusion.3
  32.0 3.3 %fusion = f32[576]{0:T(1024)S(1)} fusion(bf16[576,3584]{1,0:T(8,128)(2,1)} %param.14), kind=kLoop, calls=%fused_computation.12 | loop fusion | flops 6192576 | bytes 4131072 | tf_op jit(solution)/shard_map/reduce_sum | solution.py:18
  35.4 1.3 fusion.14
  36.7 1.9 %gather_fusion.1 = bf16[768,128]{1,0:T(8,128)(2,1)S(1)} fusion(bf16[576,128]{1,0:T(8,128)(2,1)S(1)} %fusion.14, s32[1024]{0:T(1024)S(1)} %pad_clamp_fusion), kind=kCustom, calls=%fused_computation.1 | custom fusion | bytes 396288 | tf_op jit(solution)/shard_map/gather | solution.py:172
  38.6 3.5 %fusion.17 = f32[576,1,128]{2,0,1:T(8,128)S(1)} fusion(bf16[3584,128]{1,0:T(8,128)(2,1)S(1)} %copy-done.10, f32[128]{0:T(128)S(1)} %copy-done.14, bf16[576,3584]{1,0:T(8,128)(2,1)} %param.14, f32[3584]{0:T(1024)S(1)} %copy-done.11, f32[576]{0:T(1024)S(1)} %add_rsqrt_fusion), kind=kOutput, calls=%fused_computation.43 | convolution fusion | flops 536961024 | bytes 5358336 | tf_op jit(solution)/shard_map/dot_general | solution.py:58
  42.1 1.6 fusion.32
  43.9 1.9 %gather_fusion.2 = bf16[768,128]{1,0:T(8,128)(2,1)S(1)} fusion(bf16[576,128]{1,0:T(8,128)(2,1)S(1)} %pad_maximum_fusion.1, s32[1024]{0:T(1024)S(1)} %pad_clamp_fusion), kind=kCustom, calls=%fused_computation.2 | custom fusion | bytes 396288 | tf_op jit(solution)/shard_map/gather | solution.py:172
  45.8 5.6 %fusion.7 = f32[576,512]{1,0:T(8,128)S(1)} fusion(bf16[3584,512]{1,0:T(8,128)(2,1)} %param.20, f32[512]{0:T(512)S(1)} %copy-done.12, bf16[576,3584]{1,0:T(8,128)(2,1)} %param.14, f32[3584]{0:T(1024)S(1)} %copy-done.11, f32[576]{0:T(1024)S(1)} %add_rsqrt_fusion), kind=kOutput, calls=%fused_computation.27 | convolution fusion | flops 2123071488 | bytes 8997120 | tf_op jit(solution)/shard_map/dot_general | solution.py:55
  51.4 0.9 broadcast_select_fusion.1
  52.4 6.0 %all-to-all-start.2 = ((bf16[8,96,128]{2,1,0:T(8,128)(2,1)}), bf16[8,96,128]{2,1,0:T(8,128)(2,1)}, u32[]{:S(2)}, u32[]{:S(2)}) async-start(bf16[8,96,128]{2,1,0:T(8,128)(2,1)} %get-tuple-element.15), calls=%async_computation.2 | async-start | bytes 393216 | tf_op jit(solution)/shard_map/all_to_all | solution.py:178
  58.4 2.4 %fusion.27 = (f32[576,64]{1,0:T(8,128)}, f32[576,64]{1,0:T(8,128)}) fusion(f32[64]{0:T(128)S(1)} %multiply_exponential_fusion, s32[576]{0:T(1024)S(1)} %get-tuple-element.3, s32[576]{0:T(1024)S(1)} %get-tuple-element.4, s32[576]{0:T(1024)S(1)} %get-tuple-element.2, pred[64]{0:T(512)(128)(4,1)S(1)} %get-tuple-element.21, pred[64]{0:T(512)(128)(4,1)S(1)} %get-tuple-element.22), kind=kLoop, calls=%fused_computation.59 | loop fusion | flops 147456 | bytes 302208 | tf_op jit(solution)/shard_map/cos | solution.py:36
  61.2 1.9 %subtract_convert_fusion = (bf16[576,4,64]{2,1,0:T(4,128)(2,1)S(1)}, bf16[576,4,64]{2,1,0:T(4,128)(2,1)S(1)}) fusion(f32[576,4,128]{2,1,0:T(4,128)S(1)} %reshape.703, f32[576,64]{1,0:T(8,128)} %get-tuple-element.12, f32[576,64]{1,0:T(8,128)} %get-tuple-element.11), kind=kLoop, calls=%fused_computation.37 | loop fusion | flops 1179648 | bytes 2064384 | tf_op jit(solution)/shard_map/convert.5
  63.1 3.2 %all-to-all-done.2 = bf16[8,96,128]{2,1,0:T(8,128)(2,1)} async-done(((bf16[8,96,128]{2,1,0:T(8,128)(2,1)}), bf16[8,96,128]{2,1,0:T(8,128)(2,1)}, u32[]{:S(2)}, u32[]{:S(2)}) %all-to-all-start.2) | async-done | bytes 196640 | tf_op jit(solution)/shard_map/all_to_all | solution.py:178
  66.3 3.4 %all-to-all-start.1 = ((bf16[8,96,128]{2,1,0:T(8,128)(2,1)}), bf16[8,96,128]{2,1,0:T(8,128)(2,1)S(1)}, u32[]{:S(2)}, u32[]{:S(2)}) async-start(bf16[8,96,128]{2,1,0:T(8,128)(2,1)} %get-tuple-element.16), calls=%async_computation.1 | async-start | bytes 393216 | tf_op jit(solution)/shard_map/all_to_all | solution.py:179
  69.7 0.8 pad_maximum_fusion
  70.6 2.7 %gather_fusion.3 = bf16[768,512]{1,0:T(8,128)(2,1)S(1)} fusion(bf16[576,512]{1,0:T(8,128)(2,1)S(1)} %bitcast.115, s32[1024]{0:T(1024)S(1)} %pad_clamp_fusion), kind=kCustom, calls=%fused_computation.3 | custom fusion | bytes 1575936 | tf_op jit(solution)/shard_map/gather | solution.py:172
  73.3 1.1 broadcast_select_fusion
  74.3 3.1 %all-to-all-done.1 = bf16[8,96,128]{2,1,0:T(8,128)(2,1)S(1)} async-done(((bf16[8,96,128]{2,1,0:T(8,128)(2,1)}), bf16[8,96,128]{2,1,0:T(8,128)(2,1)S(1)}, u32[]{:S(2)}, u32[]{:S(2)}) %all-to-all-start.1) | async-done | bytes 196640 | tf_op jit(solution)/shard_map/all_to_all | solution.py:179
  77.4 3.5 %all-to-all-start.3 = ((bf16[8,96,512]{2,1,0:T(8,128)(2,1)}), bf16[8,96,512]{2,1,0:T(8,128)(2,1)S(1)}, u32[]{:S(2)}, u32[]{:S(2)}) async-start(bf16[8,96,512]{2,1,0:T(8,128)(2,1)} %broadcast_select_fusion), calls=%async_computation.3 | async-start | bytes 1572864 | tf_op jit(solution)/shard_map/all_to_all | solution.py:177
  81.6 0.6 iota_compare_fusion.5
  83.3 0.7 reduce.20
  84.2 4.6 %scatter_custom_fusion.3 = bf16[768,128]{1,0:T(8,128)(2,1)S(1)} fusion(s32[768]{0:T(1024)S(1)} %fusion.42, bf16[768,128]{1,0:T(8,128)(2,1)} %bitcast.15, bf16[]{:T(256)} %constant.28.clone.1), kind=kCustom, calls=%fused_computation.78 | custom fusion | bytes 197120 | tf_op jit(solution)/shard_map/scatter | solution.py:81
  88.8 4.3 %scatter_custom_fusion.2 = bf16[768,128]{1,0:T(8,128)(2,1)S(1)} fusion(s32[768]{0:T(1024)S(1)} %fusion.42, bf16[768,128]{1,0:T(8,128)(2,1)S(1)} %bitcast.127, bf16[]{:T(256)} %constant.28.clone.1), kind=kCustom, calls=%fused_computation.80 | custom fusion | bytes 196610 | tf_op jit(solution)/shard_map/scatter | solution.py:81
  93.1 0.6 slice.109
  93.7 0.6 slice.110
  94.4 4.0 %all-to-all-done.3 = bf16[8,96,512]{2,1,0:T(8,128)(2,1)S(1)} async-done(((bf16[8,96,512]{2,1,0:T(8,128)(2,1)}), bf16[8,96,512]{2,1,0:T(8,128)(2,1)S(1)}, u32[]{:S(2)}, u32[]{:S(2)}) %all-to-all-start.3) | async-done | bytes 786464 | tf_op jit(solution)/shard_map/all_to_all | solution.py:177
  98.3 6.2 %scatter_custom_fusion.4 = bf16[768,512]{1,0:T(8,128)(2,1)S(1)} fusion(s32[768]{0:T(1024)S(1)} %fusion.42, bf16[768,512]{1,0:T(8,128)(2,1)S(1)} %bitcast.120, bf16[]{:T(256)} %constant.28.clone.1), kind=kCustom, calls=%fused_computation.55 | custom fusion | bytes 786434 | tf_op jit(solution)/shard_map/scatter | solution.py:81
  104.9 1.3 fusion.54
  106.6 0.5 fusion.12
  108.6 0.9 fusion.9
  109.7 7.4 %convolution_convert_fusion = bf16[768,3584]{1,0:T(8,128)(2,1)} fusion(bf16[512,3584]{1,0:T(8,128)(2,1)} %param.26, bf16[384,512]{1,0:T(8,128)(2,1)S(1)} %bitcast.125, bf16[384,512]{1,0:T(8,128)(2,1)S(1)} %copy.76), kind=kOutput, calls=%fused_computation.15 | convolution fusion | flops 2822897664 | bytes 9961472 | tf_op jit(solution)/shard_map/dot_general | solution.py:188
  117.1 0.7 copy-done.3
  117.7 0.6 reduce_sum.49
  119.0 19.9 %psum.7 = f32[]{:T(128)} all-reduce(f32[]{:T(128)S(6)} %convert_element_type.103), channel_id=1, replica_groups=mesh['dp'=8,'seq'=4] {'dp'}, use_global_device_ids=true, to_apply=%region_16.17 | all-reduce | flops 1 | bytes 8 | tf_op jit(solution)/shard_map/psum | solution.py:160
  139.9 4.4 %scatter_custom_fusion.5 = s32[4,768]{0,1:T(8,128)S(1)} fusion(s32[768]{0:T(1024)} %copy-done.4, s32[768,4]{1,0:T(8,128)S(1)} %copy.78, s32[]{:T(128)} %constant.26.clone.1), kind=kCustom, calls=%fused_computation.65 | custom fusion | bytes 12800 | tf_op jit(solution)/shard_map/scatter | solution.py:163
  144.5 0.7 multiply_reduce_fusion
  145.1 24.1 %reduce-scatter.2.cloned.1.call-done = bf16[192,3584]{1,0:T(8,128)(2,1)} async-done(((bf16[768,3584]{1,0:T(8,128)(2,1)}), bf16[192,3584]{1,0:T(8,128)(2,1)}) %reduce-scatter.2.cloned.1.call-update) | async-done | bytes 1376272 | tf_op jit(solution)/shard_map/reduce_scatter | solution.py:187
  (81 shorter events, 6.2 us)
Async XLA Ops:
  7.2 28.2 %copy-start = (bf16[3584,128]{1,0:T(8,128)(2,1)S(1)}, bf16[3584,128]{1,0:T(8,128)(2,1)}, u32[]{:S(2)}) copy-start(bf16[3584,128]{1,0:T(8,128)(2,1)} %param.22) | copy-start | bytes 2752516
  22.2 13.1 %copy-start.11 = (f32[3584]{0:T(1024)S(1)}, f32[3584]{0:T(1024)}, u32[]{:S(2)}) copy-start(f32[3584]{0:T(1024)} %param.19) | copy-start | bytes 43012
  22.2 13.1 %copy-start.13 = (f32[128]{0:T(128)S(1)}, f32[128]{0:T(128)}, u32[]{:S(2)}) copy-start(f32[128]{0:T(128)} %param.25) | copy-start | bytes 1540
  23.8 28.6 %all-to-all-start = ((s32[8,1,480]{2,1,0:T(1,128)}), s32[8,1,480]{2,1,0:T(1,128)S(1)}, u32[]{:S(2)}, u32[]{:S(2)}) async-start(s32[8,1,480]{2,1,0:T(1,128)} %reshape.820), calls=%async_computation | async-start | bytes 32768 | tf_op jit(solution)/shard_map/all_to_all | solution.py:159
  31.1 4.3 %copy-start.1 = (bf16[576,3584]{1,0:T(8,128)(2,1)S(1)}, bf16[576,3584]{1,0:T(8,128)(2,1)}, u32[]{:S(2)}) copy-start(bf16[576,3584]{1,0:T(8,128)(2,1)} %param.14) | copy-start | bytes 12386308
  35.4 3.2 %copy-start.10 = (bf16[3584,128]{1,0:T(8,128)(2,1)S(1)}, bf16[3584,128]{1,0:T(8,128)(2,1)}, u32[]{:S(2)}) copy-start(bf16[3584,128]{1,0:T(8,128)(2,1)} %param.21) | copy-start | bytes 2752516
  35.4 3.2 %copy-start.14 = (f32[128]{0:T(128)S(1)}, f32[128]{0:T(128)}, u32[]{:S(2)}) copy-start(f32[128]{0:T(128)} %param.24) | copy-start | bytes 1540
  42.1 3.7 %copy-start.12 = (f32[512]{0:T(512)S(1)}, f32[512]{0:T(512)}, u32[]{:S(2)}) copy-start(f32[512]{0:T(512)} %param.23) | copy-start | bytes 6148
  52.4 13.9 %all-to-all-start.2 = ((bf16[8,96,128]{2,1,0:T(8,128)(2,1)}), bf16[8,96,128]{2,1,0:T(8,128)(2,1)}, u32[]{:S(2)}, u32[]{:S(2)}) async-start(bf16[8,96,128]{2,1,0:T(8,128)(2,1)} %get-tuple-element.15), calls=%async_computation.2 | async-start | bytes 393216 | tf_op jit(solution)/shard_map/all_to_all | solution.py:178
  66.3 11.1 %all-to-all-start.1 = ((bf16[8,96,128]{2,1,0:T(8,128)(2,1)}), bf16[8,96,128]{2,1,0:T(8,128)(2,1)S(1)}, u32[]{:S(2)}, u32[]{:S(2)}) async-start(bf16[8,96,128]{2,1,0:T(8,128)(2,1)} %get-tuple-element.16), calls=%async_computation.1 | async-start | bytes 393216 | tf_op jit(solution)/shard_map/all_to_all | solution.py:179
  73.3 7.7 %copy-start.5 = (s32[8,3]{0,1:T(4,128)S(1)}, s32[8,3]{0,1:T(4,128)}, u32[]{:S(2)}) copy-start(s32[8,3]{0,1:T(4,128)} %param.17) | copy-start | bytes 292
  77.4 21.0 %all-to-all-start.3 = ((bf16[8,96,512]{2,1,0:T(8,128)(2,1)}), bf16[8,96,512]{2,1,0:T(8,128)(2,1)S(1)}, u32[]{:S(2)}, u32[]{:S(2)}) async-start(bf16[8,96,512]{2,1,0:T(8,128)(2,1)} %broadcast_select_fusion), calls=%async_computation.3 | async-start | bytes 1572864 | tf_op jit(solution)/shard_map/all_to_all | solution.py:177
  80.9 88.3 %reduce-scatter.2.cloned.1.call-start = ((), (), s32[]{:S(2)}) async-start(), calls=%async_computation.5 | async-start | bytes 6881280 | tf_op jit(solution)/shard_map/reduce_scatter | solution.py:187
  82.2 6.6 %copy-start.8 = (pred[384]{0:T(512)(128)(4,1)}, pred[384]{0:T(512)(128)(4,1)S(1)}, u32[]{:S(2)}) copy-start(pred[384]{0:T(512)(128)(4,1)S(1)} %iota_compare_fusion.5) | copy-start | bytes 1156
  82.5 6.3 %copy-start.6 = (pred[2,192]{1,0:T(4,128)(4,1)}, pred[2,192]{1,0:T(4,128)(4,1)S(1)}, u32[]{:S(2)}) copy-start(pred[2,192]{1,0:T(4,128)(4,1)S(1)} %iota_compare_fusion.4) | copy-start | bytes 1156
  84.1 14.2 %copy-start.4 = (s32[768]{0:T(1024)}, s32[768]{0:T(1024)S(1)}, u32[]{:S(2)}) copy-start(s32[768]{0:T(1024)S(1)} %fusion.42) | copy-start | bytes 9220
  104.8 1.7 copy-start.2
  104.8 1.7 copy-start.7
  107.5 1.1 copy-start.9
  117.0 0.7 copy-start.3
Sparse Core Ops, SparseCore 0:
  117.2 52.0 reduce-scatter.1
where the time goes:
time: 177 us; the launch traced here: 176 us
  local copies, waits for them, and re-layouts  44 us (25%)
  waiting for transfers between devices  34.3 us (19%)
  matrix products  21.1 us (12%)
  other arithmetic  20.5 us (12%)
  starting transfers between devices  20.3 us (11%)
  blocking collectives  19.9 us (11%)
  between operations  15.9 us (9%)
    reduce_scatter x1, waiting for transfers between devices, per_device(): lax.psum_scatter(jnp.dot(context, o_weight, preferred_element_type=jnp.fl...  24.1 us
    psum x1, blocking collectives, per_device(): loss_total = lax.psum(mask_sum.astype(jnp.float32), 'dp')  19.9 us
    scatter x3, local copies, waits for them, and re-layouts, place_rows(): return empty.at[target_slots].set(flat_rows, mode='drop')  15.1 us
    dot_general x1, matrix products, per_device(): jnp.dot(context, o_weight, preferred_element_type=jnp.float32)  7.37 us
    all_to_all x1, starting transfers between devices, per_device(): lax.all_to_all(send_info, 'dp', split_axis=1, concat_axis=1, tiled=True)  7.28 us
    gather x3, local copies, waits for them, and re-layouts, select_slots(): source_array[source_of]  6.44 us
    all_to_all x1, starting transfers between devices, per_device(): lax.all_to_all(select_slots(k_all), 'dp', split_axis=0, concat_axis=0, ti...  5.99 us
    dot_general x1, matrix products, project(): jnp.dot(normed, q_weight, preferred_element_type=jnp.float32) + q_bias  5.64 us
  transfers between devices with their start and end apart: 5, of which 4 were waited for; matrix products, arithmetic and copies ran while one was open for 28% of the time, Pallas kernels for 0%

commit v1 on v0

v1 whole, which is shorter than its diff:
```python
import functools
import math

import jax
import jax.numpy as jnp
from jax import lax
from jax.experimental import pallas as pl
from jax.experimental.pallas import tpu as pltpu
from jax.sharding import PartitionSpec as P

DH = 128
BUCKET = 384
LANES = 128

NORM_EPSILON = 1e-06
ROPE_BASE = 1000000.0
F32 = jnp.float32
BF16 = jnp.bfloat16


def rotary_tables(position_ids, head_size):
    half_size = head_size // 2
    pair_index = jnp.arange(head_size, dtype=jnp.int32) % half_size
    inv_freq = jnp.exp(pair_index.astype(F32) * (-2.0 * math.log(ROPE_BASE) / head_size))
    time_limit = head_size // 8
    height_limit = time_limit + 3 * head_size // 16
    chosen = jnp.where(
        pair_index[None, :] < time_limit,
        position_ids[0][:, None],
        jnp.where(
            pair_index[None, :] < height_limit, position_ids[1][:, None], position_ids[2][:, None]
        ),
    )
    angles = chosen.astype(F32) * inv_freq[None, :]
    sign = jnp.where(jnp.arange(head_size) < half_size, -1.0, 1.0).astype(F32)
    return (jnp.cos(angles), jnp.sin(angles) * sign[None, :])


def iota(shape, axis):
    return lax.broadcasted_iota(jnp.int32, shape, axis)


def project_kernel(
    peers, slot_count, room, group, head_count, depth,
    tok_ref, gain_ref, qw_ref, kw_ref, vw_ref, bias_ref, cos_ref, sin_ref, slot_ref, mask_ref,
    packed_ref, info_ref, acc, squares, turned,
):
    step = pl.program_id(0)
    rows = tok_ref.shape[0]
    width = acc.shape[1]

    @pl.when(step == 0)
    def _():
        acc[...] = jnp.zeros_like(acc)
        squares[...] = jnp.zeros_like(squares)

    x = tok_ref[...].astype(F32)
    sq = x * x
    part = sq[:, :LANES]
    for i in range(1, x.shape[1] // LANES):
        part = part + sq[:, i * LANES : (i + 1) * LANES]
    squares[...] += part
    scaled = (x * gain_ref[...]).astype(BF16)
    weights = jnp.concatenate([qw_ref[...], kw_ref[...], vw_ref[...]], axis=1)
    acc[...] += jnp.dot(scaled, weights, preferred_element_type=F32)

    @pl.when(step == pl.num_programs(0) - 1)
    def _():
        mean_square = jnp.sum(squares[...], axis=1, keepdims=True) * (1.0 / depth)
        inverse = lax.rsqrt(mean_square + NORM_EPSILON)
        cosine = cos_ref[...]
        sine = sin_ref[...]
        for h in range(width // DH):
            cols = slice(h * DH, (h + 1) * DH)
            head = (acc[:, cols] * inverse + bias_ref[:, cols]).astype(BF16)
            if h < head_count:
                wide = head.astype(F32)
                head = (wide * cosine + pltpu.roll(wide, DH // 2, 1) * sine).astype(BF16)
            turned[:, cols] = head
        slots = slot_ref[...]
        peer = slots // slot_count
        local = slots - peer * slot_count + 1
        mask = mask_ref[...].astype(F32)
        mask_sum = jnp.sum(mask, axis=1, keepdims=True)
        hot = jnp.where(iota((peers, rows), 0) == peer, 1.0, 0.0)
        earlier = jnp.where(iota((rows, rows), 0) < iota((rows, rows), 1), 1.0, 0.0).astype(BF16)
        counts = jnp.dot(hot.astype(BF16), earlier, preferred_element_type=F32)
        rank = jnp.sum(hot * counts, axis=0, keepdims=True).astype(jnp.int32)
        place = peer * LANES + rank
        high = local // 32
        kind = iota((8, rows), 0)
        facts = jnp.where(
            kind == 0,
            high.astype(F32),
            jnp.where(
                kind == 1, (local - high * 32).astype(F32), jnp.where(kind == 2, mask, 0.0)
            ),
        ).astype(BF16)
        values = turned[...]
        span = group * LANES
        for g in range(peers // group):
            select = jnp.where(iota((span, rows), 0) + g * span == place, 1.0, 0.0).astype(BF16)
            moved = jnp.dot(select, values, preferred_element_type=F32).astype(BF16)
            told = lax.dot_general(
                facts, select, (((1,), (1,)), ((), ())), preferred_element_type=F32
            )
            told = jnp.where(iota(told.shape, 0) == 3, mask_sum, told)
            for p in range(group):
                packed_ref[g * group + p] = moved[p * LANES : p * LANES + room]
                info_ref[g * group + p] = told[:, p * LANES : (p + 1) * LANES]


def attend(kv_slots, lengths, head_count, ctx):
    start = 0
    scale = 1.0 / math.sqrt(DH)
    for size, length in zip((BUCKET, BUCKET // 2, BUCKET // 2), lengths):
        rows = slice(start, start + size)
        key = kv_slots[rows, head_count * DH : (head_count + 1) * DH]
        value = kv_slots[rows, (head_count + 1) * DH : (head_count + 2) * DH]
        q_at, k_at = iota((size, size), 0), iota((size, size), 1)
        allowed = (q_at >= k_at) & (k_at < length)
        live = iota((size, DH), 0) < length
        for h in range(head_count):
            cols = slice(h * DH, (h + 1) * DH)
            scores = lax.dot_general(
                kv_slots[rows, cols], key, (((1,), (1,)), ((), ())), preferred_element_type=F32
            )
            scores = jnp.where(allowed, scores * scale, -1e30)
            top = jnp.max(scores, axis=1, keepdims=True)
            weights = jnp.exp(scores - top)
            total = jnp.sum(weights, axis=1, keepdims=True)
            out = jnp.dot(weights.astype(BF16), value, preferred_element_type=F32) / total
            ctx[rows, cols] = jnp.where(live, out, 0.0).astype(BF16)
        start += size


def exchange_kernel(
    peers, group, seq_count, source_rows, head_count, chunk,
    packed_ref, info_ref, tokens_ref, ow_hbm,
    mixed_ref, weight_ref,
    got, got_info, select, padded, slots, ctx, ow, own,
    near_out, near_in, mine_out, mine_in, far_out, far_in,
    data_send, data_recv, info_send, info_recv, near_send, near_recv,
    mine_send, mine_recv, far_send, far_recv, ow_sem,
):
    me = lax.axis_index("dp")
    seat = lax.axis_index("seq")
    half = seat // 2
    core = seat % 2
    partner = half * 2 + (1 - core)
    across = (1 - half) * 2 + core
    room = packed_ref.shape[1]
    slot_count = slots.shape[0]
    part = slot_count // seq_count
    chunks = ow.shape[1] // chunk

    load = pltpu.make_async_copy(ow_hbm, ow, ow_sem)
    load.start()
    barrier = pltpu.get_barrier_semaphore()
    for d in range(1, peers):
        pl.semaphore_signal(barrier, inc=1, device_id={"dp": (me + d) % peers})
    pl.semaphore_signal(barrier, inc=1, device_id={"seq": partner})
    pl.semaphore_signal(barrier, inc=1, device_id={"seq": across})
    pl.semaphore_wait(barrier, peers + 1)

    def sends(d):
        to = (me + d) % peers
        return (
            pltpu.make_async_remote_copy(
                info_ref.at[to], got_info.at[me], info_send.at[d], info_recv.at[d],
                device_id={"dp": to},
            ),
            pltpu.make_async_remote_copy(
                packed_ref.at[to], got.at[me], data_send.at[d], data_recv.at[d],
                device_id={"dp": to},
            ),
        )

    for d in range(1, peers):
        for copy in sends(d):
            copy.start()
    got[me] = packed_ref[me]
    got_info[me] = info_ref[me]
    padded[...] = jnp.zeros_like(padded)
    for d in range(1, peers):
        for copy in sends(d):
            copy.wait()

    count = jnp.zeros((1, LANES), F32)
    seen = jnp.zeros((8, part), F32)
    placed = jnp.zeros(slots.shape, F32)
    slot_at = iota((slot_count, LANES), 0).astype(F32)
    for g in range(peers // group):
        facts = []
        for p in range(group):
            told = got_info[g * group + p]
            facts.append(told)
            count = count + told[3:4]
            local = told[0:1] * 32.0 + told[1:2] - 1.0
            select[:, p * LANES : (p + 1) * LANES] = jnp.where(
                slot_at == local, 1.0, 0.0
            ).astype(BF16)
            padded[p * LANES : p * LANES + room, :] = got[g * group + p]
        flags = jnp.concatenate(facts, axis=1).astype(BF16)
        own_select = select[pl.ds(pl.multiple_of(seat * part, part), part), :]
        seen = seen + lax.dot_general(
            flags, own_select, (((1,), (1,)), ((), ())), preferred_element_type=F32
        )
        placed = placed + jnp.dot(select[...], padded[...], preferred_element_type=F32)
    slots[...] = placed.astype(BF16)
    weight_ref[...] = seen[2:3] * ((peers * source_rows) / count[:, :1])

    lengths = [tokens_ref[me, i] for i in range(3)]
    attend(slots, lengths, head_count, ctx)
    load.wait()

    def block(index):
        return ctx[pl.ds(pl.multiple_of(index * part, part), part), :]

    def near_copy(j):
        return pltpu.make_async_remote_copy(
            near_out.at[j], near_in.at[j], near_send.at[j], near_recv.at[j],
            device_id={"seq": partner},
        )

    def mine_copy(j):
        return pltpu.make_async_remote_copy(
            mine_out.at[j], mine_in.at[j], mine_send.at[j], mine_recv.at[j],
            device_id={"seq": partner},
        )

    def far_copy(j):
        return pltpu.make_async_remote_copy(
            far_out.at[j], far_in.at[j], far_send.at[j], far_recv.at[j],
            device_id={"seq": across},
        )

    held = [None] * chunks

    def forward(j):
        near_copy(j).wait()
        far_out[j] = (held[j] + near_in[j].astype(F32)).astype(BF16)
        far_copy(j).start()

    for j in range(chunks):
        w = ow[:, j * chunk : (j + 1) * chunk]
        near_out[j] = jnp.dot(
            block((1 - half) * 2 + (1 - core)), w, preferred_element_type=F32
        ).astype(BF16)
        near_copy(j).start()
        held[j] = jnp.dot(block(across), w, preferred_element_type=F32)
        if j > 0:
            forward(j - 1)
    forward(chunks - 1)
    for j in range(chunks):
        w = ow[:, j * chunk : (j + 1) * chunk]
        mine_out[j] = jnp.dot(block(partner), w, preferred_element_type=F32).astype(BF16)
        mine_copy(j).start()
        own[:, j * chunk : (j + 1) * chunk] = jnp.dot(
            block(seat), w, preferred_element_type=F32
        )
    for j in range(chunks):
        mine_copy(j).wait()
        cols = slice(j * chunk, (j + 1) * chunk)
        own[:, cols] += mine_in[j].astype(F32)
    for j in range(chunks):
        far_copy(j).wait()
        cols = slice(j * chunk, (j + 1) * chunk)
        mixed_ref[:, cols] = (own[:, cols] + far_in[j].astype(F32)).astype(BF16)


def per_device(
    tokens, positions, loss_mask, sample_tokens, dest_slot, norm_gain,
    q_weight, k_weight, v_weight, q_bias, k_bias, v_bias, o_weight,
):
    peers = lax.axis_size("dp")
    seq_count = lax.axis_size("seq")
    rows, depth = tokens.shape
    slot_count = 2 * BUCKET
    room = -(-(slot_count // peers) // 16) * 16
    group = math.gcd(peers, 8)
    q_heads = q_weight.shape[1] // DH
    kv_heads = k_weight.shape[1] // DH
    width = (q_heads + 2 * kv_heads) * DH
    chunk = math.gcd(depth, 512)
    part = slot_count // seq_count
    out_width = o_weight.shape[1]
    out_chunk = math.gcd(out_width, 512)
    out_chunks = out_width // out_chunk
    cosine, sine = rotary_tables(positions, DH)
    bias = jnp.concatenate([q_bias, k_bias, v_bias])[None, :]
    whole = lambda *shape: pl.BlockSpec(shape, lambda k: (0,) * len(shape))
    packed, info = pl.pallas_call(
        functools.partial(
            project_kernel, peers, slot_count, room, group, q_heads + kv_heads, depth
        ),
        grid=(depth // chunk,),
        in_specs=[
            pl.BlockSpec((rows, chunk), lambda k: (0, k)),
            pl.BlockSpec((1, chunk), lambda k: (0, k)),
            pl.BlockSpec((chunk, q_heads * DH), lambda k: (k, 0)),
            pl.BlockSpec((chunk, kv_heads * DH), lambda k: (k, 0)),
            pl.BlockSpec((chunk, kv_heads * DH), lambda k: (k, 0)),
            whole(1, width),
            whole(rows, DH),
            whole(rows, DH),
            whole(1, rows),
            whole(1, rows),
        ],
        out_specs=[whole(peers, room, width), whole(peers, 8, LANES)],
        out_shape=[
            jax.ShapeDtypeStruct((peers, room, width), BF16),
            jax.ShapeDtypeStruct((peers, 8, LANES), F32),
        ],
        scratch_shapes=[
            pltpu.VMEM((rows, width), F32),
            pltpu.VMEM((rows, LANES), F32),
            pltpu.VMEM((rows, width), BF16),
        ],
        compiler_params=pltpu.CompilerParams(vmem_limit_bytes=56 * 2**20),
    )(
        tokens, norm_gain[None, :], q_weight, k_weight, v_weight, bias, cosine, sine,
        dest_slot[None, :], loss_mask[None, :],
    )
    vmem = pl.BlockSpec(memory_space=pltpu.VMEM)
    piece = pltpu.VMEM((out_chunks, part, out_chunk), BF16)
    dma = pltpu.SemaphoreType.DMA
    mixed, weight = pl.pallas_call(
        functools.partial(
            exchange_kernel, peers, group, seq_count, rows, q_heads, out_chunk
        ),
        in_specs=[
            vmem,
            vmem,
            pl.BlockSpec(memory_space=pltpu.SMEM),
            pl.BlockSpec(memory_space=pl.ANY),
        ],
        out_specs=[vmem, vmem],
        out_shape=[
            jax.ShapeDtypeStruct((part, out_width), BF16),
            jax.ShapeDtypeStruct((1, part), F32),
        ],
        scratch_shapes=[
            pltpu.VMEM((peers, room, width), BF16),
            pltpu.VMEM((peers, 8, LANES), F32),
            pltpu.VMEM((slot_count, group * LANES), BF16),
            pltpu.VMEM((group * LANES, width), BF16),
            pltpu.VMEM((slot_count, width), BF16),
            pltpu.VMEM((slot_count, q_heads * DH), BF16),
            pltpu.VMEM(o_weight.shape, BF16),
            pltpu.VMEM((part, out_width), F32),
            piece, piece, piece, piece, piece, piece,
            dma((peers,)), dma((peers,)), dma((peers,)), dma((peers,)),
            dma((out_chunks,)), dma((out_chunks,)), dma((out_chunks,)),
            dma((out_chunks,)), dma((out_chunks,)), dma((out_chunks,)),
            dma,
        ],
        compiler_params=pltpu.CompilerParams(
            collective_id=0, has_side_effects=True, vmem_limit_bytes=56 * 2**20
        ),
    )(packed, info, sample_tokens, o_weight)
    return (mixed, weight.reshape(part))


def solution(mesh):
    return jax.shard_map(
        per_device,
        mesh=mesh,
        in_specs=(
            P("dp", None),
            P(None, "dp"),
            P("dp"),
            P(),
            P("dp"),
            P(),
            P(None, "seq"),
            P(None, "seq"),
            P(None, "seq"),
            P("seq"),
            P("seq"),
            P("seq"),
            P("seq", None),
        ),
        out_specs=(P(("dp", "seq"), None), P(("dp", "seq"))),
        check_vma=False,
    )
```

time: 177 us -> 98 us (0.55)
  the two profiles are of different devices: /device:TPU:0 before, /device:TPU:10 now
where the time goes in v1:
time: 98 us; the launch traced here: 97.5 us
  Pallas kernels  83.3 us (85%)
  local copies, waits for them, and re-layouts  10.4 us (11%)
  other arithmetic  3.15 us (3%)
    pallas_call x1, Pallas kernels, per_device(): pl.pallas_call(functools.partial(exchange_kernel, peers, group, seq_count...  71.8 us
    pallas_call x1, Pallas kernels, per_device(): pl.pallas_call(functools.partial(project_kernel, peers, slot_count, room,...  11.6 us
    unnamed x3, local copies, waits for them, and re-layouts  5.08 us
    mul x1, other arithmetic, rotary_tables(): return (jnp.cos(angles), jnp.sin(angles) * sign[None, :])  2.42 us

profile of v1, /device:TPU:10, one launch (start us, length us, event | category | flops | bytes accessed | tf_op | source)
XLA Modules:
  0.0 97.5 jit_solution(8034257718594534017)
XLA Ops:
  0.7 1.3 %broadcast_in_dim.83.mask_ref = s32[1,576]{1,0:T(1,128)} reshape(s32[576]{0:T(1024)} %param.15) | data formatting | bytes 4608 | tf_op jit(solution)/shard_map/broadcast_in_dim | solution.py:323
  1.9 1.3 %broadcast_in_dim.82.slot_ref = s32[1,576]{1,0:T(1,128)} reshape(s32[576]{0:T(1024)} %param.17) | data formatting | bytes 4608 | tf_op jit(solution)/shard_map/broadcast_in_dim | solution.py:323
  3.2 1.3 %copy.15.tokens_ref = s32[8,3]{1,0:T(8,128)} copy(s32[8,3]{0,1:T(4,128)} %param.16) | data formatting | bytes 192 | tf_op args[3]
  4.5 0.7 pad_maximum_fusion
  5.3 0.6 broadcast_in_dim.71.bias_ref
  5.9 0.8 slice_reduce_fusion.2
  6.7 1.3 %broadcast_in_dim.70.gain_ref = f32[1,3584]{1,0:T(1,128)} reshape(f32[3584]{0:T(1024)} %param.18) | data formatting | bytes 28672 | tf_op jit(solution)/shard_map/broadcast_in_dim | solution.py:322
  8.0 2.4 %sine_multiply_fusion = (f32[576,128]{1,0:T(8,128)}, f32[576,128]{1,0:T(8,128)}) fusion(f32[128]{0:T(128)S(1)} %get-tuple-element.15, f32[128]{0:T(128)S(1)} %get-tuple-element.16, s32[576]{0:T(1024)S(1)} %get-tuple-element.11, s32[576]{0:T(1024)S(1)} %get-tuple-element.12, s32[576]{0:T(1024)S(1)} %get-tuple-element.10, ...), kind=kLoop, calls=%fused_computation | loop fusion | flops 368640 | bytes 598016 | tf_op jit(solution)/shard_map/mul | solution.py:36
  10.4 11.6 %shard_map.140 = (bf16[8,96,768]{2,1,0:T(8,128)(2,1)}, f32[8,8,128]{2,1,0:T(8,128)}) custom-call(bf16[576,3584]{1,0:T(8,128)(2,1)} %tok_ref.1, f32[1,3584]{1,0:T(1,128)} %broadcast_in_dim.70.gain_ref, bf16[3584,512]{1,0:T(8,128)(2,1)} %qw_ref.1, bf16[3584,128]{1,0:T(8,128)(2,1)} %kw_ref.1, bf16[3584,128]{1,0:T(8,128)(2,1)} %vw_ref.1, ...), custom_call_target="tpu_custom_call" | custom-call | tf_op jit(solution)/shard_map/pallas_call | solution.py:293
  22.0 71.8 %shard_map.141 = (bf16[192,3584]{1,0:T(8,128)(2,1)}, f32[1,192]{1,0:T(1,128)}) custom-call(bf16[8,96,768]{2,1,0:T(8,128)(2,1)} %get-tuple-element.6.packed_ref, f32[8,8,128]{2,1,0:T(8,128)} %get-tuple-element.7.info_ref, s32[8,3]{1,0:T(8,128)} %copy.15.tokens_ref, bf16[512,3584]{1,0:T(8,128)(2,1)} %ow_hbm.1), custom_call_target="tpu_custom_call" | custom-call | tf_op jit(solution)/shard_map/pallas_call | solution.py:328
  93.8 2.5 %copy.18 = bf16[192,3584]{1,0:T(8,128)(2,1)} copy(bf16[192,3584]{1,0:T(8,128)(2,1)} %get-tuple-element.21) | data formatting | bytes 2752512
  96.3 1.2 %copy.19 = f32[192]{0:T(256)} copy(f32[192]{0:T(256)} %bitcast.1) | data formatting | bytes 1536
  (2 shorter events, 0.0 us)

commit v2 on v1

v2 whole, which is shorter than its diff:
```python
import functools
import math

import jax
import jax.numpy as jnp
from jax import lax
from jax.experimental import pallas as pl
from jax.experimental.pallas import tpu as pltpu
from jax.sharding import PartitionSpec as P

DH = 128
BUCKET = 384
LANES = 128

NORM_EPSILON = 1e-06
ROPE_BASE = 1000000.0
F32 = jnp.float32
BF16 = jnp.bfloat16


def rotary_tables(position_ids, head_size):
    half_size = head_size // 2
    pair_index = jnp.arange(head_size, dtype=jnp.int32) % half_size
    inv_freq = jnp.exp(pair_index.astype(F32) * (-2.0 * math.log(ROPE_BASE) / head_size))
    time_limit = head_size // 8
    height_limit = time_limit + 3 * head_size // 16
    chosen = jnp.where(
        pair_index[None, :] < time_limit,
        position_ids[0][:, None],
        jnp.where(
            pair_index[None, :] < height_limit, position_ids[1][:, None], position_ids[2][:, None]
        ),
    )
    angles = chosen.astype(F32) * inv_freq[None, :]
    sign = jnp.where(jnp.arange(head_size) < half_size, -1.0, 1.0).astype(F32)
    return (jnp.cos(angles), jnp.sin(angles) * sign[None, :])


def iota(shape, axis):
    return lax.broadcasted_iota(jnp.int32, shape, axis)


def pack_plan(peers, slot_count, group, slot_ref, mask_ref, select_out, info_out):
    rows = slot_ref.shape[0]
    slots = slot_ref[...][None, :]
    peer = slots // slot_count
    local = slots - peer * slot_count + 1
    mask = mask_ref[...][None, :].astype(F32)
    mask_sum = jnp.sum(mask, axis=1, keepdims=True)
    hot = jnp.where(iota((peers, rows), 0) == peer, 1.0, 0.0)
    earlier = jnp.where(iota((rows, rows), 0) < iota((rows, rows), 1), 1.0, 0.0).astype(BF16)
    counts = jnp.dot(hot.astype(BF16), earlier, preferred_element_type=F32)
    rank = jnp.sum(hot * counts, axis=0, keepdims=True).astype(jnp.int32)
    place = peer * LANES + rank
    high = local // 32
    kind = iota((8, rows), 0)
    facts = jnp.where(
        kind == 0,
        high.astype(F32),
        jnp.where(kind == 1, (local - high * 32).astype(F32), jnp.where(kind == 2, mask, 0.0)),
    ).astype(BF16)
    span = group * LANES
    for g in range(peers // group):
        select = jnp.where(iota((span, rows), 0) + g * span == place, 1.0, 0.0).astype(BF16)
        select_out[g * span : (g + 1) * span, :] = select
        told = lax.dot_general(facts, select, (((1,), (1,)), ((), ())), preferred_element_type=F32)
        told = jnp.where(iota(told.shape, 0) == 3, mask_sum, told)
        for p in range(group):
            info_out[g * group + p] = told[:, p * LANES : (p + 1) * LANES]


def attend(q_slots, kv_slots, lengths, heads, per_kv, kv_count, ctx):
    start = 0
    scale = 1.0 / math.sqrt(DH)
    for size, length in zip((BUCKET, BUCKET // 2, BUCKET // 2), lengths):
        rows = slice(start, start + size)
        q_at, k_at = iota((size, size), 0), iota((size, size), 1)
        allowed = (q_at >= k_at) & (k_at < length)
        live = iota((size, DH), 0) < length
        for h in heads:
            pair = h // per_kv
            key = kv_slots[rows, pair * DH : (pair + 1) * DH]
            value = kv_slots[rows, (kv_count + pair) * DH : (kv_count + pair + 1) * DH]
            cols = slice(h * DH, (h + 1) * DH)
            scores = lax.dot_general(
                q_slots[rows, cols], key, (((1,), (1,)), ((), ())), preferred_element_type=F32
            )
            scores = jnp.where(allowed, scores * scale, -1e30)
            top = jnp.max(scores, axis=1, keepdims=True)
            weights = jnp.exp(scores - top)
            total = jnp.sum(weights, axis=1, keepdims=True)
            out = jnp.dot(weights.astype(BF16), value, preferred_element_type=F32) / total
            ctx[rows, cols] = jnp.where(live, out, 0.0).astype(BF16)
        start += size


def layer_kernel(
    peers, group, seq_count, q_heads, kv_heads, chunk, room, strips,
    tok_hbm, gain_ref, qw_hbm, kw_hbm, vw_hbm, qb_ref, kb_ref, vb_ref, cos_ref, sin_ref,
    slot_ref, mask_ref, tokens_ref, ow_hbm,
    mixed_ref, weight_ref,
    x, squares, qw, kvw, ow, pick, told_out, got_info, q_out, q_got, kv_out, kv_got,
    select, padded, q_slots, kv_slots, ctx, own,
    near_out, near_in, mine_out, mine_in, far_out, far_in,
    data_send, data_recv, info_send, info_recv, near_send, near_recv,
    mine_send, mine_recv, far_send, far_recv, load_sem,
):
    me = lax.axis_index("dp")
    seat = lax.axis_index("seq")
    half = seat // 2
    core = seat % 2
    partner = half * 2 + (1 - core)
    across = (1 - half) * 2 + core
    rows, depth = x.shape
    slot_count = q_slots.shape[0]
    part = slot_count // seq_count
    chunks = ow.shape[1] // chunk
    strip = rows // strips
    kv_cols = kv_heads * DH

    barrier = pltpu.get_barrier_semaphore()
    for d in range(1, peers):
        pl.semaphore_signal(barrier, inc=1, device_id={"dp": (me + d) % peers})
    pl.semaphore_signal(barrier, inc=1, device_id={"seq": partner})
    pl.semaphore_signal(barrier, inc=1, device_id={"seq": across})
    token_loads = [
        pltpu.make_async_copy(
            tok_hbm.at[i * strip : (i + 1) * strip], x.at[i * strip : (i + 1) * strip],
            load_sem.at[i],
        )
        for i in range(strips)
    ]
    k_load = pltpu.make_async_copy(kw_hbm, kvw.at[:, :kv_cols], load_sem.at[strips])
    v_load = pltpu.make_async_copy(vw_hbm, kvw.at[:, kv_cols:], load_sem.at[strips + 1])
    q_load = pltpu.make_async_copy(qw_hbm, qw, load_sem.at[strips + 2])
    o_load = pltpu.make_async_copy(ow_hbm, ow, load_sem.at[strips + 3])
    for copy in token_loads + [k_load, v_load, q_load, o_load]:
        copy.start()

    pack_plan(peers, slot_count, group, slot_ref, mask_ref, pick, told_out)
    gain = gain_ref[...][None, :]
    for i in range(strips):
        token_loads[i].wait()
        at = slice(i * strip, (i + 1) * strip)
        total = jnp.zeros((strip, LANES), F32)
        for c in range(depth // LANES):
            cols = slice(c * LANES, (c + 1) * LANES)
            wide = x[at, cols].astype(F32)
            total = total + wide * wide
            x[at, cols] = (wide * gain[:, cols]).astype(BF16)
        squares[at, :] = jnp.sum(total, axis=1, keepdims=True)
    inverse = lax.rsqrt(squares[...] * (1.0 / depth) + NORM_EPSILON)

    def info_copy(d):
        to = (me + d) % peers
        return pltpu.make_async_remote_copy(
            told_out.at[to], got_info.at[me], info_send.at[d], info_recv.at[d],
            device_id={"dp": to},
        )

    def data_copy(stage, d):
        to = (me + d) % peers
        source, target = (kv_out, kv_got) if stage == 0 else (q_out, q_got)
        if stage > 0:
            source, target = source.at[stage - 1], target.at[stage - 1]
        return pltpu.make_async_remote_copy(
            source.at[to], target.at[me], data_send.at[stage, d], data_recv.at[stage, d],
            device_id={"dp": to},
        )

    def turn(wide):
        return wide * cos_ref[...] + pltpu.roll(wide, DH // 2, 1) * sin_ref[...]

    def pack(stage, values):
        span = group * LANES
        target, kept = (kv_out, kv_got) if stage == 0 else (q_out, q_got)
        if stage > 0:
            target, kept = target.at[stage - 1], kept.at[stage - 1]
        for g in range(peers // group):
            moved = jnp.dot(
                pick[g * span : (g + 1) * span, :], values, preferred_element_type=F32
            ).astype(BF16)
            for p in range(group):
                target[g * group + p] = moved[p * LANES : p * LANES + room]
        for d in range(1, peers):
            data_copy(stage, d).start()
        kept[me] = target[me]

    pl.semaphore_wait(barrier, peers + 1)
    for d in range(1, peers):
        info_copy(d).start()
    got_info[me] = told_out[me]
    k_load.wait()
    v_load.wait()
    product = jnp.dot(x[...], kvw[...], preferred_element_type=F32)
    pieces = []
    for h in range(2 * kv_heads):
        bias_ref, at = (kb_ref, h) if h < kv_heads else (vb_ref, h - kv_heads)
        bias = bias_ref[at * DH : (at + 1) * DH][None, :]
        head = (product[:, h * DH : (h + 1) * DH] * inverse + bias).astype(BF16)
        if h < kv_heads:
            head = turn(head.astype(F32)).astype(BF16)
        pieces.append(head)
    pack(0, jnp.concatenate(pieces, axis=1))
    q_load.wait()
    q_stages = q_out.shape[0]
    per_stage = q_heads // q_stages
    for stage in range(q_stages):
        cols = slice(stage * per_stage * DH, (stage + 1) * per_stage * DH)
        product = jnp.dot(x[...], qw[:, cols], preferred_element_type=F32)
        pieces = []
        for i in range(per_stage):
            h = stage * per_stage + i
            bias = qb_ref[h * DH : (h + 1) * DH][None, :]
            head = (product[:, i * DH : (i + 1) * DH] * inverse + bias).astype(BF16)
            pieces.append(turn(head.astype(F32)).astype(BF16))
        pack(stage + 1, jnp.concatenate(pieces, axis=1))

    padded[...] = jnp.zeros_like(padded)
    for d in range(1, peers):
        info_copy(d).wait()
    count = jnp.zeros((1, LANES), F32)
    slot_at = iota((slot_count, LANES), 0).astype(F32)
    facts = []
    for p in range(peers):
        told = got_info[p]
        facts.append(told)
        count = count + told[3:4]
        local = told[0:1] * 32.0 + told[1:2] - 1.0
        select[:, p * LANES : (p + 1) * LANES] = jnp.where(slot_at == local, 1.0, 0.0).astype(BF16)
    flags = jnp.concatenate(facts, axis=1).astype(BF16)
    own_select = select[pl.ds(pl.multiple_of(seat * part, part), part), :]
    seen = lax.dot_general(flags, own_select, (((1,), (1,)), ((), ())), preferred_element_type=F32)
    weight_ref[...] = seen[2:3] * ((peers * rows) / count[:, :1])

    def place(stage):
        for d in range(1, peers):
            data_copy(stage, d).wait()
        source = kv_got if stage == 0 else q_got.at[stage - 1]
        width = source.shape[2]
        for p in range(peers):
            padded[p * LANES : p * LANES + room, :width] = source[p]
        return jnp.dot(select[...], padded[:, :width], preferred_element_type=F32).astype(BF16)

    mine = tokens_ref[pl.ds(me, 1), :]
    lengths = [mine[:, i : i + 1] for i in range(3)]
    kv_slots[...] = place(0)
    for stage in range(q_stages):
        cols = slice(stage * per_stage * DH, (stage + 1) * per_stage * DH)
        q_slots[:, cols] = place(stage + 1)
        heads = range(stage * per_stage, (stage + 1) * per_stage)
        attend(q_slots, kv_slots, lengths, heads, q_heads // kv_heads, kv_heads, ctx)
    o_load.wait()

    def block(index):
        return ctx[pl.ds(pl.multiple_of(index * part, part), part), :]

    def near_copy(j):
        return pltpu.make_async_remote_copy(
            near_out.at[j], near_in.at[j], near_send.at[j], near_recv.at[j],
            device_id={"seq": partner},
        )

    def mine_copy(j):
        return pltpu.make_async_remote_copy(
            mine_out.at[j], mine_in.at[j], mine_send.at[j], mine_recv.at[j],
            device_id={"seq": partner},
        )

    def far_copy(j):
        return pltpu.make_async_remote_copy(
            far_out.at[j], far_in.at[j], far_send.at[j], far_recv.at[j],
            device_id={"seq": across},
        )

    held = [None] * chunks

    def forward(j):
        near_copy(j).wait()
        far_out[j] = (held[j] + near_in[j].astype(F32)).astype(BF16)
        far_copy(j).start()

    for j in range(chunks):
        w = ow[:, j * chunk : (j + 1) * chunk]
        near_out[j] = jnp.dot(
            block((1 - half) * 2 + (1 - core)), w, preferred_element_type=F32
        ).astype(BF16)
        near_copy(j).start()
        held[j] = jnp.dot(block(across), w, preferred_element_type=F32)
        if j > 0:
            forward(j - 1)
    forward(chunks - 1)
    for j in range(chunks):
        w = ow[:, j * chunk : (j + 1) * chunk]
        mine_out[j] = jnp.dot(block(partner), w, preferred_element_type=F32).astype(BF16)
        mine_copy(j).start()
        own[:, j * chunk : (j + 1) * chunk] = jnp.dot(
            block(seat), w, preferred_element_type=F32
        )
    for j in range(chunks):
        mine_copy(j).wait()
        cols = slice(j * chunk, (j + 1) * chunk)
        own[:, cols] += mine_in[j].astype(F32)
    for j in range(chunks):
        far_copy(j).wait()
        cols = slice(j * chunk, (j + 1) * chunk)
        mixed_ref[:, cols] = (own[:, cols] + far_in[j].astype(F32)).astype(BF16)


def per_device(
    tokens, positions, loss_mask, sample_tokens, dest_slot, norm_gain,
    q_weight, k_weight, v_weight, q_bias, k_bias, v_bias, o_weight,
):
    peers = lax.axis_size("dp")
    seq_count = lax.axis_size("seq")
    rows, depth = tokens.shape
    slot_count = 2 * BUCKET
    room = -(-(slot_count // peers) // 16) * 16
    group = math.gcd(peers, 8)
    q_heads = q_weight.shape[1] // DH
    kv_heads = k_weight.shape[1] // DH
    per_stage = math.gcd(q_heads, 2)
    stages = q_heads // per_stage
    strips = math.gcd(rows // 16, 4)
    part = slot_count // seq_count
    out_width = o_weight.shape[1]
    chunk = math.gcd(out_width, 512)
    chunks = out_width // chunk
    kv_width = 2 * kv_heads * DH
    q_width = per_stage * DH
    cosine, sine = rotary_tables(positions, DH)
    vmem = pl.BlockSpec(memory_space=pltpu.VMEM)
    hbm = pl.BlockSpec(memory_space=pl.ANY)
    piece = pltpu.VMEM((chunks, part, chunk), BF16)
    dma = pltpu.SemaphoreType.DMA
    mixed, weight = pl.pallas_call(
        functools.partial(
            layer_kernel, peers, group, seq_count, q_heads, kv_heads, chunk, room, strips
        ),
        in_specs=[
            hbm, vmem, hbm, hbm, hbm, vmem, vmem, vmem, vmem, vmem, vmem, vmem, vmem, hbm,
        ],
        out_specs=[vmem, vmem],
        out_shape=[
            jax.ShapeDtypeStruct((part, out_width), BF16),
            jax.ShapeDtypeStruct((1, part), F32),
        ],
        scratch_shapes=[
            pltpu.VMEM((rows, depth), BF16),
            pltpu.VMEM((rows, 1), F32),
            pltpu.VMEM(q_weight.shape, BF16),
            pltpu.VMEM((depth, kv_width), BF16),
            pltpu.VMEM(o_weight.shape, BF16),
            pltpu.VMEM((peers * LANES, rows), BF16),
            pltpu.VMEM((peers, 8, LANES), F32),
            pltpu.VMEM((peers, 8, LANES), F32),
            pltpu.VMEM((stages, peers, room, q_width), BF16),
            pltpu.VMEM((stages, peers, room, q_width), BF16),
            pltpu.VMEM((peers, room, kv_width), BF16),
            pltpu.VMEM((peers, room, kv_width), BF16),
            pltpu.VMEM((slot_count, peers * LANES), BF16),
            pltpu.VMEM((peers * LANES, max(kv_width, q_width)), BF16),
            pltpu.VMEM((slot_count, q_heads * DH), BF16),
            pltpu.VMEM((slot_count, kv_width), BF16),
            pltpu.VMEM((slot_count, q_heads * DH), BF16),
            pltpu.VMEM((part, out_width), F32),
            piece, piece, piece, piece, piece, piece,
            dma((stages + 1, peers)), dma((stages + 1, peers)), dma((peers,)), dma((peers,)),
            dma((chunks,)), dma((chunks,)), dma((chunks,)),
            dma((chunks,)), dma((chunks,)), dma((chunks,)),
            dma((strips + 4,)),
        ],
        compiler_params=pltpu.CompilerParams(
            collective_id=0, has_side_effects=True, vmem_limit_bytes=67043328
        ),
    )(
        tokens, norm_gain, q_weight, k_weight, v_weight, q_bias, k_bias, v_bias, cosine, sine,
        dest_slot, loss_mask, sample_tokens, o_weight,
    )
    return (mixed, weight.reshape(part))


def solution(mesh):
    return jax.shard_map(
        per_device,
        mesh=mesh,
        in_specs=(
            P("dp", None),
            P(None, "dp"),
            P("dp"),
            P(),
            P("dp"),
            P(),
            P(None, "seq"),
            P(None, "seq"),
            P(None, "seq"),
            P("seq"),
            P("seq"),
            P("seq"),
            P("seq", None),
        ),
        out_specs=(P(("dp", "seq"), None), P(("dp", "seq"))),
        check_vma=False,
    )
```

time: 98 us -> 83.6 us (0.85)
  the two profiles are of different devices: /device:TPU:10 before, /device:TPU:0 now
where the time goes in v2:
time: 83.6 us; the launch traced here: 83.3 us
  Pallas kernels  74.3 us (89%)
  local copies, waits for them, and re-layouts  5.92 us (7%)
  other arithmetic  2.48 us (3%)
    pallas_call x1, Pallas kernels, per_device(): pl.pallas_call(functools.partial(layer_kernel, peers, group, seq_count, q...  74.3 us
    unnamed x3, local copies, waits for them, and re-layouts  5.08 us
    mul x1, other arithmetic, rotary_tables(): return (jnp.cos(angles), jnp.sin(angles) * sign[None, :])  2.46 us

profile of v2, /device:TPU:0, one launch (start us, length us, event | category | flops | bytes accessed | tf_op | source)
XLA Modules:
  0.0 83.3 jit_solution(753540218948981117)
XLA Ops:
  0.7 1.4 %copy.15.tokens_ref = s32[8,3]{1,0:T(8,128)} copy(s32[8,3]{0,1:T(4,128)} %param.16) | data formatting | bytes 192 | tf_op args[3]
  2.0 0.8 %slice_reduce_fusion.2 = (s32[576]{0:T(1024)S(1)}, s32[576]{0:T(1024)S(1)}, s32[576]{0:T(1024)S(1)}) fusion(s32[3,576]{1,0:T(4,128)} %param.14), kind=kLoop, calls=%fused_computation.5 | loop fusion | bytes 13824 | tf_op jit(solution)/shard_map/slice | solution.py:29
  2.8 2.5 %sine_multiply_fusion = (f32[576,128]{1,0:T(8,128)}, f32[576,128]{1,0:T(8,128)}) fusion(f32[128]{0:T(128)S(1)} %get-tuple-element.11, f32[128]{0:T(128)S(1)} %get-tuple-element.12, s32[576]{0:T(1024)S(1)} %get-tuple-element.7, s32[576]{0:T(1024)S(1)} %get-tuple-element.8, s32[576]{0:T(1024)S(1)} %get-tuple-element.6, pred[128]{0:T(512)(128)(4,1)S(1)} %get-tuple-element.13, ...), kind=kLoop, calls=%fused_computation | loop fusion | flops 368640 | bytes 598016 | tf_op jit(solution)/shard_map/mul | solution.py:36
  5.3 74.3 %shard_map.140 = (bf16[192,3584]{1,0:T(8,128)(2,1)}, f32[1,192]{1,0:T(1,128)}) custom-call(bf16[576,3584]{1,0:T(8,128)(2,1)} %tok_hbm.1, f32[3584]{0:T(1024)} %gain_ref.1, bf16[3584,512]{1,0:T(8,128)(2,1)} %qw_hbm.1, bf16[3584,128]{1,0:T(8,128)(2,1)} %kw_hbm.1, bf16[3584,128]{1,0:T(8,128)(2,1)} %vw_hbm.1, f32[512]{0:T(512)} %qb_ref.1, f32[128]{0:T(128)} %kb_ref.1, ...), custom_call_target="tpu_custom_call" | custom-call | tf_op jit(solution)/shard_map/pallas_call | solution.py:336
  79.6 2.5 %copy.18 = bf16[192,3584]{1,0:T(8,128)(2,1)} copy(bf16[192,3584]{1,0:T(8,128)(2,1)} %get-tuple-element.17) | data formatting | bytes 2752512
  82.1 1.2 %copy.19 = f32[192]{0:T(256)} copy(f32[192]{0:T(256)} %bitcast.1) | data formatting | bytes 1536
  (2 shorter events, 0.0 us)

commit v3 on v2

--- a/solution.py
+++ b/solution.py
@@ -18,26 +18,36 @@
 BF16 = jnp.bfloat16
 
 
-def rotary_tables(position_ids, head_size):
-    half_size = head_size // 2
-    pair_index = jnp.arange(head_size, dtype=jnp.int32) % half_size
-    inv_freq = jnp.exp(pair_index.astype(F32) * (-2.0 * math.log(ROPE_BASE) / head_size))
-    time_limit = head_size // 8
-    height_limit = time_limit + 3 * head_size // 16
-    chosen = jnp.where(
-        pair_index[None, :] < time_limit,
-        position_ids[0][:, None],
-        jnp.where(
-            pair_index[None, :] < height_limit, position_ids[1][:, None], position_ids[2][:, None]
-        ),
-    )
-    angles = chosen.astype(F32) * inv_freq[None, :]
-    sign = jnp.where(jnp.arange(head_size) < half_size, -1.0, 1.0).astype(F32)
-    return (jnp.cos(angles), jnp.sin(angles) * sign[None, :])
-
-
 def iota(shape, axis):
     return lax.broadcasted_iota(jnp.int32, shape, axis)
+
+
+def rotary_tables(pos_ref, cos_out, sin_out):
+    ids = pos_ref[...]
+    rows = ids.shape[1]
+    high = ids // 32
+    low = ids - high * 32
+    kind = iota((8, rows), 0)
+    split = jnp.zeros((8, rows), jnp.int32)
+    for axis in range(3):
+        split = jnp.where(kind == 2 * axis, high[axis : axis + 1], split)
+        split = jnp.where(kind == 2 * axis + 1, low[axis : axis + 1], split)
+    half_size = DH // 2
+    lane, row = iota((8, DH), 1), iota((8, DH), 0)
+    pair = lane % half_size
+    time_limit = DH // 8
+    height_limit = time_limit + 3 * DH // 16
+    axis = jnp.where(pair < time_limit, 0, jnp.where(pair < height_limit, 1, 2))
+    pick = jnp.where(row == 2 * axis, 32.0, jnp.where(row == 2 * axis + 1, 1.0, 0.0))
+    chosen = lax.dot_general(
+        split.astype(F32).astype(BF16), pick.astype(BF16), (((0,), (0,)), ((), ())),
+        preferred_element_type=F32,
+    )
+    turn_at = iota((1, DH), 1)
+    power = (turn_at % half_size).astype(F32)
+    angles = chosen * jnp.exp(power * (-2.0 * math.log(ROPE_BASE) / DH))
+    cos_out[...] = jnp.cos(angles)
+    sin_out[...] = jnp.sin(angles) * jnp.where(turn_at < half_size, -1.0, 1.0)
 
 
 def pack_plan(peers, slot_count, group, slot_ref, mask_ref, select_out, info_out):
@@ -96,14 +106,15 @@
 
 def layer_kernel(
     peers, group, seq_count, q_heads, kv_heads, chunk, room, strips,
-    tok_hbm, gain_ref, qw_hbm, kw_hbm, vw_hbm, qb_ref, kb_ref, vb_ref, cos_ref, sin_ref,
-    slot_ref, mask_ref, tokens_ref, ow_hbm,
+    tok_hbm, gain_ref, qw_hbm, kw_hbm, vw_hbm, qb_ref, kb_ref, vb_ref, pos_ref,
+    slot_ref, mask_ref, ow_hbm,
     mixed_ref, weight_ref,
     x, squares, qw, kvw, ow, pick, told_out, got_info, q_out, q_got, kv_out, kv_got,
     select, padded, q_slots, kv_slots, ctx, own,
-    near_out, near_in, mine_out, mine_in, far_out, far_in,
+    near_out, near_in, mine_out, mine_in, far_out, far_in, cos_ref, sin_ref, wide, ctx_all,
     data_send, data_recv, info_send, info_recv, near_send, near_recv,
-    mine_send, mine_recv, far_send, far_recv, load_sem,
+    mine_send, mine_recv, far_send, far_recv, load_sem, wide_load_sem,
+    wide_send, wide_recv, ctx_send, ctx_recv,
 ):
     me = lax.axis_index("dp")
     seat = lax.axis_index("seq")
@@ -111,10 +122,14 @@
     core = seat % 2
     partner = half * 2 + (1 - core)
     across = (1 - half) * 2 + core
+    q_stages = q_out.shape[0]
+    per_stage = q_heads // q_stages
     rows, depth = x.shape
     slot_count = q_slots.shape[0]
     part = slot_count // seq_count
+    wides = wide.shape[1]
     chunks = ow.shape[1] // chunk
+    diagonal = (1 - half) * 2 + (1 - core)
     strip = rows // strips
     kv_cols = kv_heads * DH
 
@@ -123,6 +138,7 @@
         pl.semaphore_signal(barrier, inc=1, device_id={"dp": (me + d) % peers})
     pl.semaphore_signal(barrier, inc=1, device_id={"seq": partner})
     pl.semaphore_signal(barrier, inc=1, device_id={"seq": across})
+    pl.semaphore_signal(barrier, inc=1, device_id={"seq": diagonal})
     token_loads = [
         pltpu.make_async_copy(
             tok_hbm.at[i * strip : (i + 1) * strip], x.at[i * strip : (i + 1) * strip],
@@ -133,11 +149,18 @@
     k_load = pltpu.make_async_copy(kw_hbm, kvw.at[:, :kv_cols], load_sem.at[strips])
     v_load = pltpu.make_async_copy(vw_hbm, kvw.at[:, kv_cols:], load_sem.at[strips + 1])
     q_load = pltpu.make_async_copy(qw_hbm, qw, load_sem.at[strips + 2])
-    o_load = pltpu.make_async_copy(ow_hbm, ow, load_sem.at[strips + 3])
-    for copy in token_loads + [k_load, v_load, q_load, o_load]:
+    o_load = pltpu.make_async_copy(ow_hbm.at[:, wides * chunk :], ow, load_sem.at[strips + 3])
+    wide_loads = [
+        pltpu.make_async_copy(
+            ow_hbm.at[:, i * chunk : (i + 1) * chunk], wide.at[seat, i], wide_load_sem.at[i]
+        )
+        for i in range(wides)
+    ]
+    for copy in token_loads + [k_load, v_load] + wide_loads + [q_load, o_load]:
         copy.start()
 
     pack_plan(peers, slot_count, group, slot_ref, mask_ref, pick, told_out)
+    rotary_tables(pos_ref, cos_ref, sin_ref)
     gain = gain_ref[...][None, :]
     for i in range(strips):
         token_loads[i].wait()
@@ -145,9 +168,9 @@
         total = jnp.zeros((strip, LANES), F32)
         for c in range(depth // LANES):
             cols = slice(c * LANES, (c + 1) * LANES)
-            wide = x[at, cols].astype(F32)
-            total = total + wide * wide
-            x[at, cols] = (wide * gain[:, cols]).astype(BF16)
+            entry = x[at, cols].astype(F32)
+            total = total + entry * entry
+            x[at, cols] = (entry * gain[:, cols]).astype(BF16)
         squares[at, :] = jnp.sum(total, axis=1, keepdims=True)
     inverse = lax.rsqrt(squares[...] * (1.0 / depth) + NORM_EPSILON)
 
@@ -156,6 +179,26 @@
         return pltpu.make_async_remote_copy(
             told_out.at[to], got_info.at[me], info_send.at[d], info_recv.at[d],
             device_id={"dp": to},
+        )
+
+    def wide_copy(kind, i):
+        index = across if kind == 2 else seat
+        return pltpu.make_async_remote_copy(
+            wide.at[index, i], wide.at[index, i], wide_send.at[kind, i], wide_recv.at[kind, i],
+            device_id={"seq": across if kind == 1 else partner},
+        )
+
+    def pass_on(i):
+        wide_copy(1, i).wait()
+        wide_copy(2, i).start()
+
+    def ctx_copy(stage, kind):
+        to = (partner, across, diagonal)[kind]
+        cols = slice(stage * per_stage * DH, (stage + 1) * per_stage * DH)
+        return pltpu.make_async_remote_copy(
+            ctx.at[pl.ds(pl.multiple_of(to * part, part), part), cols],
+            ctx_all.at[seat, :, cols], ctx_send.at[stage, kind], ctx_recv.at[stage, kind],
+            device_id={"seq": to},
         )
 
     def data_copy(stage, d):
@@ -186,10 +229,14 @@
             data_copy(stage, d).start()
         kept[me] = target[me]
 
-    pl.semaphore_wait(barrier, peers + 1)
+    pl.semaphore_wait(barrier, peers + 2)
     for d in range(1, peers):
         info_copy(d).start()
     got_info[me] = told_out[me]
+    for i in range(wides):
+        wide_loads[i].wait()
+        wide_copy(1, i).start()
+        wide_copy(0, i).start()
     k_load.wait()
     v_load.wait()
     product = jnp.dot(x[...], kvw[...], preferred_element_type=F32)
@@ -203,8 +250,6 @@
         pieces.append(head)
     pack(0, jnp.concatenate(pieces, axis=1))
     q_load.wait()
-    q_stages = q_out.shape[0]
-    per_stage = q_heads // q_stages
     for stage in range(q_stages):
         cols = slice(stage * per_stage * DH, (stage + 1) * per_stage * DH)
         product = jnp.dot(x[...], qw[:, cols], preferred_element_type=F32)
@@ -222,11 +267,16 @@
     count = jnp.zeros((1, LANES), F32)
     slot_at = iota((slot_count, LANES), 0).astype(F32)
     facts = []
+    filled = [jnp.zeros((1, LANES), F32) for _ in range(3)]
+    starts = (0, BUCKET, BUCKET + BUCKET // 2, 2 * BUCKET)
     for p in range(peers):
         told = got_info[p]
         facts.append(told)
         count = count + told[3:4]
         local = told[0:1] * 32.0 + told[1:2] - 1.0
+        for b in range(3):
+            inside = (local >= float(starts[b])) & (local < float(starts[b + 1]))
+            filled[b] = filled[b] + jnp.where(inside, 1.0, 0.0)
         select[:, p * LANES : (p + 1) * LANES] = jnp.where(slot_at == local, 1.0, 0.0).astype(BF16)
     flags = jnp.concatenate(facts, axis=1).astype(BF16)
     own_select = select[pl.ds(pl.multiple_of(seat * part, part), part), :]
@@ -242,14 +292,20 @@
             padded[p * LANES : p * LANES + room, :width] = source[p]
         return jnp.dot(select[...], padded[:, :width], preferred_element_type=F32).astype(BF16)
 
-    mine = tokens_ref[pl.ds(me, 1), :]
-    lengths = [mine[:, i : i + 1] for i in range(3)]
+    lengths = [jnp.sum(one, axis=1, keepdims=True).astype(jnp.int32) for one in filled]
     kv_slots[...] = place(0)
     for stage in range(q_stages):
         cols = slice(stage * per_stage * DH, (stage + 1) * per_stage * DH)
         q_slots[:, cols] = place(stage + 1)
         heads = range(stage * per_stage, (stage + 1) * per_stage)
+        if stage == 0 and wides > 1:
+            pass_on(0)
         attend(q_slots, kv_slots, lengths, heads, q_heads // kv_heads, kv_heads, ctx)
+        for kind in range(3):
+            ctx_copy(stage, kind).start()
+        ctx_all[seat, :, cols] = ctx[pl.ds(pl.multiple_of(seat * part, part), part), cols]
+    for i in range(1, wides - 1):
+        pass_on(i)
     o_load.wait()
 
     def block(index):
@@ -290,6 +346,7 @@
         if j > 0:
             forward(j - 1)
     forward(chunks - 1)
+    pass_on(wides - 1)
     for j in range(chunks):
         w = ow[:, j * chunk : (j + 1) * chunk]
         mine_out[j] = jnp.dot(block(partner), w, preferred_element_type=F32).astype(BF16)
@@ -297,6 +354,18 @@
         own[:, j * chunk : (j + 1) * chunk] = jnp.dot(
             block(seat), w, preferred_element_type=F32
         )
+    for stage in range(q_stages):
+        for kind in range(3):
+            ctx_copy(stage, kind).wait()
+    for i in range(wides):
+        wide_copy(0, i).wait()
+        wide_copy(2, i).wait()
+        total = jnp.zeros((part, chunk), F32)
+        for index in range(seq_count):
+            total = total + jnp.dot(
+                ctx_all[index], wide[index, i], preferred_element_type=F32
+            )
+        mixed_ref[:, i * chunk : (i + 1) * chunk] = total.astype(BF16)
     for j in range(chunks):
         mine_copy(j).wait()
         cols = slice(j * chunk, (j + 1) * chunk)
@@ -304,7 +373,9 @@
     for j in range(chunks):
         far_copy(j).wait()
         cols = slice(j * chunk, (j + 1) * chunk)
-        mixed_ref[:, cols] = (own[:, cols] + far_in[j].astype(F32)).astype(BF16)
+        mixed_ref[:, (wides + j) * chunk : (wides + j + 1) * chunk] = (
+            own[:, cols] + far_in[j].astype(F32)
+        ).astype(BF16)
 
 
 def per_device(
@@ -325,10 +396,10 @@
     part = slot_count // seq_count
     out_width = o_weight.shape[1]
     chunk = math.gcd(out_width, 512)
-    chunks = out_width // chunk
+    wides = max(1, 3 * (out_width // chunk) // 7)
+    chunks = out_width // chunk - wides
     kv_width = 2 * kv_heads * DH
     q_width = per_stage * DH
-    cosine, sine = rotary_tables(positions, DH)
     vmem = pl.BlockSpec(memory_space=pltpu.VMEM)
     hbm = pl.BlockSpec(memory_space=pl.ANY)
     piece = pltpu.VMEM((chunks, part, chunk), BF16)
@@ -338,7 +409,7 @@
             layer_kernel, peers, group, seq_count, q_heads, kv_heads, chunk, room, strips
         ),
         in_specs=[
-            hbm, vmem, hbm, hbm, hbm, vmem, vmem, vmem, vmem, vmem, vmem, vmem, vmem, hbm,
+            hbm, vmem, hbm, hbm, hbm, vmem, vmem, vmem, vmem, vmem, vmem, hbm,
         ],
         out_specs=[vmem, vmem],
         out_shape=[
@@ -350,7 +421,7 @@
             pltpu.VMEM((rows, 1), F32),
             pltpu.VMEM(q_weight.shape, BF16),
             pltpu.VMEM((depth, kv_width), BF16),
-            pltpu.VMEM(o_weight.shape, BF16),
+            pltpu.VMEM((o_weight.shape[0], chunks * chunk), BF16),
             pltpu.VMEM((peers * LANES, rows), BF16),
             pltpu.VMEM((peers, 8, LANES), F32),
             pltpu.VMEM((peers, 8, LANES), F32),
@@ -363,19 +434,24 @@
             pltpu.VMEM((slot_count, q_heads * DH), BF16),
             pltpu.VMEM((slot_count, kv_width), BF16),
             pltpu.VMEM((slot_count, q_heads * DH), BF16),
-            pltpu.VMEM((part, out_width), F32),
+            pltpu.VMEM((part, chunks * chunk), F32),
             piece, piece, piece, piece, piece, piece,
+            pltpu.VMEM((rows, DH), F32),
+            pltpu.VMEM((rows, DH), F32),
+            pltpu.VMEM((seq_count, wides, o_weight.shape[0], chunk), BF16),
+            pltpu.VMEM((seq_count, part, q_heads * DH), BF16),
             dma((stages + 1, peers)), dma((stages + 1, peers)), dma((peers,)), dma((peers,)),
             dma((chunks,)), dma((chunks,)), dma((chunks,)),
             dma((chunks,)), dma((chunks,)), dma((chunks,)),
-            dma((strips + 4,)),
+            dma((strips + 4,)), dma((wides,)), dma((3, wides)), dma((3, wides)),
+            dma((stages, 3)), dma((stages, 3)),
         ],
         compiler_params=pltpu.CompilerParams(
             collective_id=0, has_side_effects=True, vmem_limit_bytes=67043328
         ),
     )(
-        tokens, norm_gain, q_weight, k_weight, v_weight, q_bias, k_bias, v_bias, cosine, sine,
-        dest_slot, loss_mask, sample_tokens, o_weight,
+        tokens, norm_gain, q_weight, k_weight, v_weight, q_bias, k_bias, v_bias, positions,
+        dest_slot, loss_mask, o_weight,
     )
     return (mixed, weight.reshape(part))
 

time: 83.6 us -> 74.6 us (0.89)
  Pallas kernels: 74.3 us -> 70 us
  other arithmetic: 2.48 us -> 0 us
  local copies, waits for them, and re-layouts: 5.92 us -> 3.74 us
    pallas_call x1, Pallas kernels: 74.3 us -> 70 us  [per_device(): pl.pallas_call(functools.partial(layer_kernel, peers, group, seq_count, q...]
    mul x1 -> x0, other arithmetic: 2.46 us -> none  [rotary_tables(): return (jnp.cos(angles), jnp.sin(angles) * sign[None, :])]
    unnamed x3 -> x2, local copies, waits for them, and re-layouts: 5.08 us -> 3.74 us
    slice x1 -> x0, local copies, waits for them, and re-layouts: 0.84 us -> none  [rotary_tables(): position_ids[0][:, None]]
where the time goes in v3:
time: 74.6 us; the launch traced here: 74.4 us
  Pallas kernels  70 us (94%)
  local copies, waits for them, and re-layouts  3.74 us (5%)
    pallas_call x1, Pallas kernels, per_device(): pl.pallas_call(functools.partial(layer_kernel, peers, group, seq_count, q...  70 us
    unnamed x2, local copies, waits for them, and re-layouts  3.74 us

profile of v3, /device:TPU:0, one launch (start us, length us, event | category | flops | bytes accessed | tf_op | source)
XLA Modules:
  0.0 74.4 jit_solution(7052332428486847499)
XLA Ops:
  0.6 70.0 %shard_map.131 = (bf16[192,3584]{1,0:T(8,128)(2,1)}, f32[1,192]{1,0:T(1,128)}) custom-call(bf16[576,3584]{1,0:T(8,128)(2,1)} %tok_hbm.1, f32[3584]{0:T(1024)} %gain_ref.1, bf16[3584,512]{1,0:T(8,128)(2,1)} %qw_hbm.1, bf16[3584,128]{1,0:T(8,128)(2,1)} %kw_hbm.1, bf16[3584,128]{1,0:T(8,128)(2,1)} %vw_hbm.1, f32[512]{0:T(512)} %qb_ref.1, f32[128]{0:T(128)} %kb_ref.1, ...), custom_call_target="tpu_custom_call" | custom-call | tf_op jit(solution)/shard_map/pallas_call | solution.py:407
  70.6 2.5 %copy.16 = bf16[192,3584]{1,0:T(8,128)(2,1)} copy(bf16[192,3584]{1,0:T(8,128)(2,1)} %get-tuple-element.8) | data formatting | bytes 2752512
  73.2 1.2 %copy.17 = f32[192]{0:T(256)} copy(f32[192]{0:T(256)} %bitcast.1) | data formatting | bytes 1536
